TPU v7x, 32 devices: a whole 2x2x4 slice. The times are simulated.
32 devices in a mesh: cfg: 2 (over y), seq: 8 (over z, core), tp: 2 (over x).
Axes of the slice: x: 2, y: 2, z: 4, core: 2. Of those that a mesh axis runs over, the one named last changes fastest.
Arguments:
- queries: bfloat16 [2, 3840, 5120], P('cfg', 'seq', 'tp'), may hold values from -5 to 5
- keys: bfloat16 [2, 3840, 5120], P('cfg', 'seq', 'tp'), may hold values from -5 to 5
- values: bfloat16 [2, 3840, 5120], P('cfg', 'seq', 'tp'), may hold values from -5 to 5
- text_keys: bfloat16 [2, 512, 5120], P('cfg', None, 'tp'), may hold values from -7.5 to 7.5
- text_values: bfloat16 [2, 512, 5120], P('cfg', None, 'tp'), may hold values from -5 to 5
- prompt_lengths: int32 [2], P('cfg'), may hold values from 64 to 512
- frame_counts: int32 [8], P('seq'), may hold values from 240 to 480
- out_weight: bfloat16 [5120, 5120], P('tp'), may hold values from -0.5 to 0.5
Outputs:
- velocity: bfloat16 [3840, 5120], P('seq', ('tp', 'cfg'))
All inputs are finite; a program needn't handle non-finite values.
Results may differ from a plain program's by a relative error of at most 0.015.
Values may be sent and summed in bfloat16 or wider, within the bound.
A program may use at most 320 MiB of HBM per device.

v0:
```python
import functools

import jax
import jax.numpy as jnp
from jax import lax
from jax.experimental import pallas as pl
from jax.experimental.pallas import tpu as pltpu
from jax.sharding import PartitionSpec as P

HEAD_DIM = 128
GUIDANCE = 5.0
RESCALE = 0.7
NEGATIVE = -1e30
LOG2E = 1.4426950408889634
CORES = 2
MESH = pl.DeviceIdType.MESH


def chunk_rows(total, limit):
    for unit in (256, 128, 16):
        for size in range(limit // unit * unit, 0, -unit):
            if total % size == 0:
                return size
    return total


def attention_kernel(
    n, chips, group, rows, text,
    q, k, v, tk, tv, counts, lengths,
    out,
    qb, kb, vb, tkb, tvb, cb, bias, tbias, ob,
    send, recv, fsend, frecv, csend, crecv, local, tlocal, osend, orecv,
):
    me = lax.axis_index("seq")
    core = lax.rem(me, CORES)
    chip = lax.div(me, CORES)
    partner = chip * CORES + (CORES - 1 - core)
    scale = LOG2E * HEAD_DIM ** (-0.5)

    def cols(owner, head):
        return pl.ds(pl.multiple_of((owner * group + head) * HEAD_DIM, HEAD_DIM), HEAD_DIM)

    def slot(index):
        return pl.ds(pl.multiple_of(index * rows, 16), rows)

    def chip_at(step):
        return lax.rem(chip + step, chips)

    def chip_back(step):
        return lax.rem(chip + chips - step, chips)

    barrier = pltpu.get_barrier_semaphore()
    for step in range(1, n):
        pl.semaphore_signal(
            barrier, inc=1, device_id={"seq": lax.rem(me + step, n)}, device_id_type=MESH
        )
    pl.semaphore_wait(barrier, n - 1)

    def count_copy(step):
        return pltpu.make_async_remote_copy(
            src_ref=counts, dst_ref=cb.at[me], send_sem=csend.at[step - 1],
            recv_sem=crecv.at[step - 1],
            device_id={"seq": lax.rem(me + step, n)}, device_id_type=MESH,
        )

    def block_copies(head, step):
        target = chip_at(step)
        device = {"seq": target * CORES + core}
        made = []
        for index, (src, dst) in enumerate(
            ((k, kb.at[head, slot(me)]), (v, vb.at[head, slot(me)]), (q, qb.at[head, chip]))
        ):
            made.append(pltpu.make_async_remote_copy(
                src_ref=src.at[:, cols(target, head)], dst_ref=dst,
                send_sem=send.at[index, head, step - 1],
                recv_sem=recv.at[index, head, step - 1],
                device_id=device, device_id_type=MESH,
            ))
        return made

    def own_copies(head):
        return [
            pltpu.make_async_copy(k.at[:, cols(chip, head)], kb.at[head, slot(me)], local.at[0, head]),
            pltpu.make_async_copy(v.at[:, cols(chip, head)], vb.at[head, slot(me)], local.at[1, head]),
            pltpu.make_async_copy(q.at[:, cols(chip, head)], qb.at[head, chip], local.at[2, head]),
            pltpu.make_async_copy(tk.at[:, cols(chip, head)], tkb.at[head], tlocal.at[0, head]),
            pltpu.make_async_copy(tv.at[:, cols(chip, head)], tvb.at[head], tlocal.at[1, head]),
        ]

    def own_forward(head):
        return [
            pltpu.make_async_remote_copy(
                src_ref=src.at[:, cols(chip, head)], dst_ref=dst.at[head, slot(me)],
                send_sem=fsend.at[index, head, 0], recv_sem=frecv.at[index, head, 0],
                device_id={"seq": partner}, device_id_type=MESH,
            )
            for index, (src, dst) in enumerate(((k, kb), (v, vb)))
        ]

    def forward(index, head, step):
        buf = (kb, vb)[index]
        where = slot(chip_back(step) * CORES + core)
        return pltpu.make_async_remote_copy(
            src_ref=buf.at[head, where], dst_ref=buf.at[head, where],
            send_sem=fsend.at[index, head, step], recv_sem=frecv.at[index, head, step],
            device_id={"seq": partner}, device_id_type=MESH,
        )

    def out_copy(head, step):
        target = chip_at(step)
        return pltpu.make_async_remote_copy(
            src_ref=ob.at[head, target], dst_ref=out.at[:, cols(chip, head)],
            send_sem=osend.at[head, step], recv_sem=orecv.at[head, step],
            device_id={"seq": target * CORES + core}, device_id_type=MESH,
        )

    def own_out(head):
        return pltpu.make_async_copy(
            ob.at[head, chip], out.at[:, cols(chip, head)], osend.at[head, 0]
        )

    for step in range(1, n):
        count_copy(step).start()

    def start_head(head, _):
        for step in range(1, chips):
            for copy in block_copies(head, step):
                copy.start()
        for copy in own_copies(head):
            copy.start()
        for copy in own_forward(head):
            copy.start()
        return 0

    lax.fori_loop(0, group, start_head, 0)

    cb[me] = counts[...]
    for step in range(1, n):
        count_copy(step).wait()
    lane = lax.broadcasted_iota(jnp.int32, (rows, HEAD_DIM), 1)
    place = lax.broadcasted_iota(jnp.int32, (rows, HEAD_DIM), 0)
    for source in range(n):
        limit = cb[source][0:1, :]
        bias[source * rows:(source + 1) * rows, :] = jnp.where(
            (lane == 0) & (place >= limit), NEGATIVE, 0.0
        ).astype(jnp.bfloat16)
    tlane = lax.broadcasted_iota(jnp.int32, (text, HEAD_DIM), 1)
    tplace = lax.broadcasted_iota(jnp.int32, (text, HEAD_DIM), 0)
    tbias[...] = jnp.where(
        (tlane == 0) & (tplace >= lengths[0:1, :]), NEGATIVE, 0.0
    ).astype(jnp.bfloat16)

    total = n * rows
    size = chunk_rows(total, 768)

    def ones(length):
        return jnp.where(
            lax.broadcasted_iota(jnp.int32, (length, HEAD_DIM), 1) == 0, 1.0, 0.0
        ).astype(jnp.bfloat16)

    def one_head(head, _):
        for copy in own_copies(head):
            copy.wait()
        for step in range(1, chips):
            made = block_copies(head, step)
            for index in range(2):
                made[index].wait()
                forward(index, head, step).start()
            made[2].wait()
        for copy in own_forward(head):
            copy.wait()
        for step in range(1, chips):
            for index in range(2):
                forward(index, head, step).wait()

        def one_block(step):
            target = chip_at(step)
            query = jnp.concatenate([qb[head, target], ones(rows)], axis=1)

            def piece(state, keys, masks, vals):
                keys = jnp.concatenate([keys, masks], axis=1)
                vals = jnp.concatenate([vals, ones(vals.shape[0])], axis=1)
                scores = lax.dot_general(
                    query, keys, (((1,), (1,)), ((), ())), preferred_element_type=jnp.float32
                )
                high = jnp.max(scores, axis=1, keepdims=True) * scale
                if state is not None:
                    high = jnp.maximum(high, state[0])
                weights = jnp.exp2(scores * scale - high).astype(jnp.bfloat16)
                mixed = jnp.dot(weights, vals, preferred_element_type=jnp.float32)
                if state is not None:
                    mixed = mixed + state[1] * jnp.exp2(state[0] - high)
                return (high, mixed)

            state = piece(None, tkb[head], tbias[...], tvb[head])
            for start in range(0, total, size):
                span = pl.ds(start, size)
                state = piece(state, kb[head, span], bias[span, :], vb[head, span])
            mixed = state[1]
            ob[head, target] = (
                mixed[:, :HEAD_DIM] / mixed[:, HEAD_DIM:HEAD_DIM + 1]
            ).astype(jnp.bfloat16)

        def far_block(step, _):
            one_block(step)
            out_copy(head, step).start()
            return 0

        lax.fori_loop(1, chips, far_block, 0)
        one_block(0)
        own_out(head).start()
        return 0

    lax.fori_loop(0, group, one_head, 0)

    def finish(head, _):
        for step in range(1, chips):
            out_copy(head, step).wait()
        own_out(head).wait()
        return 0

    lax.fori_loop(0, group, finish, 0)


def attention(queries, keys, values, text_keys, text_values, prompt_lengths, frame_counts, n):
    rows, width = queries.shape
    text = text_keys.shape[0]
    chips = n // CORES
    heads = width // HEAD_DIM
    group = heads // chips
    counts = jnp.broadcast_to(frame_counts.reshape(1, 1), (8, HEAD_DIM))
    lengths = jnp.broadcast_to(prompt_lengths.reshape(1, 1), (8, HEAD_DIM))
    bf16 = jnp.bfloat16
    total = n * rows
    hbm = pl.BlockSpec(memory_space=pl.ANY)
    vmem = pl.BlockSpec(memory_space=pltpu.VMEM)
    dma = pltpu.SemaphoreType.DMA
    return pl.pallas_call(
        functools.partial(attention_kernel, n, chips, group, rows, text),
        out_shape=jax.ShapeDtypeStruct((rows, width), bf16),
        in_specs=[hbm] * 5 + [vmem] * 2,
        out_specs=hbm,
        scratch_shapes=[
            pltpu.VMEM((group, chips, rows, HEAD_DIM), bf16),
            pltpu.VMEM((group, total, HEAD_DIM), bf16),
            pltpu.VMEM((group, total, HEAD_DIM), bf16),
            pltpu.VMEM((group, text, HEAD_DIM), bf16),
            pltpu.VMEM((group, text, HEAD_DIM), bf16),
            pltpu.VMEM((n, 8, HEAD_DIM), jnp.int32),
            pltpu.VMEM((total, HEAD_DIM), bf16),
            pltpu.VMEM((text, HEAD_DIM), bf16),
            pltpu.VMEM((group, chips, rows, HEAD_DIM), bf16),
            dma((3, group, chips - 1)),
            dma((3, group, chips - 1)),
            dma((2, group, chips)),
            dma((2, group, chips)),
            dma((n - 1,)),
            dma((n - 1,)),
            dma((3, group)),
            dma((2, group)),
            dma((group, chips)),
            dma((group, chips)),
        ],
        compiler_params=pltpu.CompilerParams(
            collective_id=0, has_side_effects=True, vmem_limit_bytes=62 * 1024 * 1024
        ),
    )(queries, keys, values, text_keys, text_values, counts, lengths)


def frame_valid(positions, counts_table, slots):
    frame_index = positions // slots
    slot_index = positions % slots
    frame_ids = jnp.arange(counts_table.shape[0], dtype=jnp.int32)
    frame_limit = jnp.sum(
        jnp.where(frame_index[:, None] == frame_ids[None, :], counts_table[None, :], 0), axis=1
    )
    return slot_index < frame_limit


def attend_block(carry, key_rows, value_rows, query_heads, key_mask):
    row_max, weight_sum, mixed_sum = carry
    head_count = query_heads.shape[1]
    key_heads = key_rows.reshape(key_rows.shape[0], head_count, HEAD_DIM)
    value_heads = value_rows.reshape(value_rows.shape[0], head_count, HEAD_DIM)
    scores = jnp.einsum(
        "qhd,khd->hqk", query_heads, key_heads, preferred_element_type=jnp.float32
    ) * HEAD_DIM ** (-0.5)
    scores = jnp.where(key_mask[None, None, :], scores, NEGATIVE)
    new_max = jnp.maximum(row_max, jnp.max(scores, axis=2))
    shrink = jnp.exp(row_max - new_max)
    weights = jnp.exp(scores - new_max[:, :, None])
    weight_sum = weight_sum * shrink + jnp.sum(weights, axis=2)
    mixed_sum = mixed_sum * shrink[:, :, None] + jnp.einsum(
        "hqk,khd->hqd",
        weights.astype(jnp.bfloat16),
        value_heads,
        preferred_element_type=jnp.float32,
    )
    return (new_max, weight_sum, mixed_sum)


def gathered_attention(
    queries, keys, values, text_keys, text_values, prompt_lengths, frame_counts, n
):
    row_count, head_cols = queries.shape
    head_count = head_cols // HEAD_DIM
    all_counts = lax.all_gather(frame_counts, "seq", axis=0, tiled=True)
    query_heads = queries.reshape(row_count, head_count, HEAD_DIM)
    text_mask = jnp.arange(text_keys.shape[0], dtype=jnp.int32) < prompt_lengths[0]
    empty_state = (
        jnp.full((head_count, row_count), NEGATIVE, jnp.float32),
        jnp.zeros((head_count, row_count), jnp.float32),
        jnp.zeros((head_count, row_count, HEAD_DIM), jnp.float32),
    )
    text_state = attend_block(empty_state, text_keys, text_values, query_heads, text_mask)
    key_rows = lax.all_gather(keys, "seq", axis=0, tiled=True)
    value_rows = lax.all_gather(values, "seq", axis=0, tiled=True)
    positions = jnp.arange(key_rows.shape[0], dtype=jnp.int32)
    _, weight_sum, mixed_sum = attend_block(
        text_state, key_rows, value_rows, query_heads,
        frame_valid(positions, all_counts, row_count // frame_counts.shape[0]),
    )
    return (
        jnp.transpose(mixed_sum / weight_sum[:, :, None], (1, 0, 2))
        .reshape(row_count, head_cols)
        .astype(jnp.bfloat16)
    )


PIECES = 5


def tail_kernel(
    n, rows, part,
    att, w, counts,
    out,
    ab, wb, sb, rb, own, yb, yr, gb, st, sg,
    asem, wsem, xsend, xrecv, ysend, yrecv, ssend, srecv,
):
    me = lax.axis_index("seq")
    t = lax.axis_index("tp")
    c = lax.axis_index("cfg")
    steps = 2 * PIECES
    width = PIECES * part

    def column(side, index):
        far = lax.div(index, PIECES)
        branch = far * c + (1 - far) * (1 - c)
        return (side * 2 + branch) * width + lax.rem(index, PIECES) * part

    def weight_copy(j):
        far = lax.div(j, steps)
        side = far * t + (1 - far) * (1 - t)
        start = pl.multiple_of(column(side, lax.rem(j, steps)), HEAD_DIM)
        return pltpu.make_async_copy(w.at[:, pl.ds(start, part)], wb.at[j], wsem.at[j])

    load = pltpu.make_async_copy(att, ab, asem)
    load.start()

    def start_weight(j, _):
        weight_copy(j).start()
        return 0

    lax.fori_loop(0, 2 * steps, start_weight, 0)

    barrier = pltpu.get_barrier_semaphore()
    pl.semaphore_signal(barrier, inc=1, device_id={"tp": 1 - t}, device_id_type=MESH)
    pl.semaphore_signal(barrier, inc=1, device_id={"cfg": 1 - c}, device_id_type=MESH)
    for step in range(1, n):
        pl.semaphore_signal(
            barrier, inc=1, device_id={"seq": lax.rem(me + step, n)}, device_id_type=MESH
        )
    pl.semaphore_wait(barrier, n + 1)

    def x_copy(i):
        return pltpu.make_async_remote_copy(
            src_ref=sb.at[i], dst_ref=rb.at[i], send_sem=xsend.at[i], recv_sem=xrecv.at[i],
            device_id={"tp": 1 - t}, device_id_type=MESH,
        )

    def y_copy(i):
        return pltpu.make_async_remote_copy(
            src_ref=yb.at[i], dst_ref=yr.at[i], send_sem=ysend.at[i], recv_sem=yrecv.at[i],
            device_id={"cfg": 1 - c}, device_id_type=MESH,
        )

    def stat_copy(step):
        return pltpu.make_async_remote_copy(
            src_ref=st, dst_ref=sg.at[me], send_sem=ssend.at[step - 1],
            recv_sem=srecv.at[step - 1],
            device_id={"seq": lax.rem(me + step, n)}, device_id_type=MESH,
        )

    load.wait()

    def project(j):
        weight_copy(j).wait()
        return jnp.dot(ab[...], wb[j], preferred_element_type=jnp.float32)

    def given(i, _):
        sb[i] = project(i).astype(jnp.bfloat16)
        x_copy(i).start()
        return 0

    def kept(i, _):
        own[i] = project(steps + i)
        return 0

    lax.fori_loop(0, steps, given, 0)
    lax.fori_loop(0, steps, kept, 0)

    def across(i, _):
        x_copy(i).wait()
        yb[i] = (own[i] + rb[i].astype(jnp.float32)).astype(jnp.bfloat16)
        y_copy(i).start()
        return 0

    lax.fori_loop(0, PIECES, across, 0)

    limit = counts[0:1, 0:1]
    valid = lax.broadcasted_iota(jnp.int32, (rows, part), 0) < limit
    first = jnp.full((rows, part), c, jnp.int32) == 0
    st[...] = jnp.zeros_like(st)
    for i in range(PIECES):
        span = pl.ds(i * part, part)
        x_copy(PIECES + i).wait()
        mine = (own[PIECES + i] + rb[PIECES + i].astype(jnp.float32)).astype(jnp.bfloat16)
        mine = mine.astype(jnp.float32)
        y_copy(i).wait()
        other = yr[i].astype(jnp.float32)
        conditional = jnp.where(first, mine, other)
        unconditional = jnp.where(first, other, mine)
        guided = unconditional + GUIDANCE * (conditional - unconditional)
        gb[:, span] = guided
        guided = jnp.where(valid, guided, 0.0)
        conditional = jnp.where(valid, conditional, 0.0)
        for row, field in enumerate(
            (guided, guided * guided, conditional, conditional * conditional)
        ):
            st[row:row + 1, span] = jnp.sum(field, axis=0, keepdims=True)
        st[4:5, span] = jnp.broadcast_to(limit.astype(jnp.float32), (1, part))

    for step in range(1, n):
        stat_copy(step).start()
    sg[me] = st[...]
    for step in range(1, n):
        stat_copy(step).wait()
    sums = sg[0]
    for source in range(1, n):
        sums = sums + sg[source]
    valid_total = sums[4:5, :]
    guided_mean = sums[0:1, :] / valid_total
    guided_var = sums[1:2, :] / valid_total - guided_mean * guided_mean
    cond_mean = sums[2:3, :] / valid_total
    cond_var = sums[3:4, :] / valid_total - cond_mean * cond_mean
    std_ratio = jnp.sqrt((cond_var + 1.0) / (guided_var + 1.0))
    factor = RESCALE * std_ratio + (1.0 - RESCALE)
    out[...] = (guided_mean + (gb[...] - guided_mean) * factor).astype(jnp.bfloat16)


def fused_tail(attended, out_weight, frame_counts, n):
    rows, depth = attended.shape
    width = out_weight.shape[1] // 4
    part = width // PIECES
    steps = 2 * PIECES
    bf16 = jnp.bfloat16
    f32 = jnp.float32
    counts = jnp.broadcast_to(frame_counts.reshape(1, 1), (8, HEAD_DIM))
    hbm = pl.BlockSpec(memory_space=pl.ANY)
    vmem = pl.BlockSpec(memory_space=pltpu.VMEM)
    dma = pltpu.SemaphoreType.DMA
    return pl.pallas_call(
        functools.partial(tail_kernel, n, rows, part),
        out_shape=jax.ShapeDtypeStruct((rows, width), bf16),
        in_specs=[hbm, hbm, vmem],
        out_specs=vmem,
        scratch_shapes=[
            pltpu.VMEM((rows, depth), bf16),
            pltpu.VMEM((2 * steps, depth, part), bf16),
            pltpu.VMEM((steps, rows, part), bf16),
            pltpu.VMEM((steps, rows, part), bf16),
            pltpu.VMEM((steps, rows, part), f32),
            pltpu.VMEM((PIECES, rows, part), bf16),
            pltpu.VMEM((PIECES, rows, part), bf16),
            pltpu.VMEM((rows, width), f32),
            pltpu.VMEM((8, width), f32),
            pltpu.VMEM((n, 8, width), f32),
            dma,
            dma((2 * steps,)),
            dma((steps,)),
            dma((steps,)),
            dma((PIECES,)),
            dma((PIECES,)),
            dma((n - 1,)),
            dma((n - 1,)),
        ],
        compiler_params=pltpu.CompilerParams(
            collective_id=1, has_side_effects=True, vmem_limit_bytes=62 * 1024 * 1024
        ),
    )(attended, out_weight, counts)


def body(n, cfgs, tps, queries, keys, values, text_keys, text_values, prompt_lengths, frame_counts, out_weight):
    rows, head_cols = queries.shape[1:]
    split = n % CORES == 0 and (head_cols // HEAD_DIM) % (n // CORES) == 0
    attend = attention if split and frame_counts.shape[0] == 1 else gathered_attention
    attended = attend(
        queries[0], keys[0], values[0], text_keys[0], text_values[0],
        prompt_lengths, frame_counts, n,
    )
    whole = out_weight.shape[1] % (4 * PIECES * HEAD_DIM) == 0
    if cfgs == 2 and tps == 2 and whole and frame_counts.shape[0] == 1:
        return fused_tail(attended, out_weight, frame_counts, n)
    branch = lax.psum_scatter(
        lax.dot_general(
            out_weight, attended, (((0,), (1,)), ((), ())), preferred_element_type=jnp.float32
        ).astype(jnp.bfloat16),
        "tp",
        scatter_dimension=0,
        tiled=True,
    )
    half = branch.shape[0] // cfgs
    mine = lax.axis_index("cfg")
    kept = lax.dynamic_slice_in_dim(branch, mine * half, half, 0)
    given = lax.dynamic_slice_in_dim(branch, (1 - mine) * half, half, 0)
    other = lax.ppermute(given, "cfg", [(0, 1), (1, 0)])
    first = mine == 0
    conditional = jnp.where(first, kept, other).astype(jnp.float32)
    unconditional = jnp.where(first, other, kept).astype(jnp.float32)
    guided = unconditional + GUIDANCE * (conditional - unconditional)
    valid = (jnp.arange(rows, dtype=jnp.int32) < frame_counts[0])[None, :]

    def local_sum(field):
        return jnp.sum(jnp.where(valid, field, 0.0), axis=1)

    sums = lax.psum(
        jnp.stack([
            local_sum(guided),
            local_sum(guided * guided),
            local_sum(conditional),
            local_sum(conditional * conditional),
            jnp.full((half,), frame_counts[0].astype(jnp.float32)),
        ]),
        "seq",
    )
    means = sums[:4] / sums[4:5]
    guided_mean = means[0]
    guided_var = means[1] - guided_mean * guided_mean
    cond_var = means[3] - means[2] * means[2]
    std_ratio = jnp.sqrt((cond_var + 1.0) / (guided_var + 1.0))
    factor = RESCALE * std_ratio + (1.0 - RESCALE)
    velocity = guided_mean[:, None] + (guided - guided_mean[:, None]) * factor[:, None]
    return velocity.astype(jnp.bfloat16).T


def solution(mesh):
    placed = (
        P("cfg", "seq", "tp"),
        P("cfg", "seq", "tp"),
        P("cfg", "seq", "tp"),
        P("cfg", None, "tp"),
        P("cfg", None, "tp"),
        P("cfg"),
        P("seq"),
        P("tp", None),
    )
    return jax.shard_map(
        functools.partial(body, mesh.shape["seq"], mesh.shape["cfg"], mesh.shape["tp"]),
        mesh=mesh, in_specs=placed, out_specs=P("seq", ("tp", "cfg")), check_vma=False,
    )
```

profile of v0, /device:TPU:0, one launch (start us, length us, event | category | flops | bytes accessed | tf_op | source)
XLA Modules:
  0.0 293.5 jit_solution(13215650715575794454)
XLA Ops:
  1.3 0.6 broadcast_in_dim.18.counts
  1.9 0.6 broadcast_in_dim.20.lengths
  2.5 218.4 %shard_map.82.att = bf16[480,2560]{1,0:T(8,128)(2,1)} custom-call(bf16[480,2560]{1,0:T(8,128)(2,1)} %bitcast.11, bf16[480,2560]{1,0:T(8,128)(2,1)} %bitcast.12, bf16[480,2560]{1,0:T(8,128)(2,1)} %bitcast.13, bf16[512,2560]{1,0:T(8,128)(2,1)} %bitcast.9, bf16[512,2560]{1,0:T(8,128)(2,1)} %bitcast.10, s32[8,128]{1,0:T(8,128)} %broadcast_in_dim.18.counts, ...), custom_call_target="tpu_custom_call" | custom-call | tf_op jit(solution)/shard_map/pallas_call | solution.py:238
  220.9 70.2 %shard_map.83 = bf16[480,1280]{1,0:T(8,128)(2,1)} custom-call(bf16[480,2560]{1,0:T(8,128)(2,1)} %shard_map.82.att, bf16[2560,5120]{1,0:T(8,128)(2,1)} %w.1, s32[8,128]{1,0:T(8,128)} %broadcast_in_dim.18.counts), custom_call_target="tpu_custom_call" | custom-call | tf_op jit(solution)/shard_map/pallas_call | solution.py:472
  291.1 2.4 copy.12
where the time goes:
time: 294 us; the launch traced here: 293 us
  Pallas kernels  289 us (98%)
  local copies, waits for them, and re-layouts  3.58 us (1%)
    pallas_call x1, Pallas kernels, attention(): pl.pallas_call(functools.partial(attention_kernel, n, chips, group, rows,...  218 us
    pallas_call x1, Pallas kernels, fused_tail(): pl.pallas_call(functools.partial(tail_kernel, n, rows, part), out_shape=j...  70.2 us

commit v1 on v0

v1 whole, which is shorter than its diff:
```python
import functools

import jax
import jax.numpy as jnp
from jax import lax
from jax.experimental import pallas as pl
from jax.experimental.pallas import tpu as pltpu
from jax.sharding import PartitionSpec as P

HEAD_DIM = 128
GUIDANCE = 5.0
RESCALE = 0.7
NEGATIVE = -1e30
LOG2E = 1.4426950408889634
CORES = 2
MESH = pl.DeviceIdType.MESH


def chunk_rows(total, limit):
    for unit in (256, 128, 16):
        for size in range(limit // unit * unit, 0, -unit):
            if total % size == 0:
                return size
    return total


def step_kernel(
    n, chips, group, rows, text, wide,
    q, k, v, tk, tv, w, counts, lengths,
    out,
    qb, kb, vb, tkb, tvb, cb, bias, tbias, ob, ab, wb, acc, st, sg,
    send, recv, fsend, frecv, csend, crecv, local, tlocal, osend, orecv,
    xsend, xrecv, ysend, yrecv, rsend, rrecv,
    wlocal, wsend, wrecv, wfsend, wfrecv, ssend, srecv,
):
    me = lax.axis_index("seq")
    t = lax.axis_index("tp")
    c = lax.axis_index("cfg")
    core = lax.rem(me, CORES)
    chip = lax.div(me, CORES)
    partner = chip * CORES + (CORES - 1 - core)
    scale = LOG2E * HEAD_DIM ** (-0.5)
    last = group - 1
    half = chips // 2
    bf16 = jnp.bfloat16
    f32 = jnp.float32

    def cols(owner, head):
        return pl.ds(pl.multiple_of((owner * group + head) * HEAD_DIM, HEAD_DIM), HEAD_DIM)

    def out_cols(side, branch):
        return pl.ds(pl.multiple_of((side * 2 + branch) * wide, HEAD_DIM), wide)

    def slot(index):
        return pl.ds(pl.multiple_of(index * rows, 16), rows)

    def chip_at(step):
        return lax.rem(chip + step, chips)

    def chip_back(step):
        return lax.rem(chip + chips - step, chips)

    def across(src, dst, sends, recvs, device):
        return pltpu.make_async_remote_copy(
            src_ref=src, dst_ref=dst, send_sem=sends, recv_sem=recvs,
            device_id=device, device_id_type=MESH,
        )

    x_side = {"tp": 1 - t}
    y_side = {"cfg": 1 - c}

    def kv_copies(head, step):
        target = chip_at(step)
        return [
            across(
                src.at[:, cols(target, head)], dst.at[head, slot(me)],
                send.at[index, head, step - 1], recv.at[index, head, step - 1],
                {"seq": target * CORES + core},
            )
            for index, (src, dst) in enumerate(((k, kb), (v, vb)))
        ]

    def q_copy(head, step):
        target = chip_at(step)
        return across(
            q.at[:, cols(target, head)], qb.at[head, chip],
            send.at[2, head, step - 1], recv.at[2, head, step - 1],
            {"seq": target * CORES + core},
        )

    def own_copies(head):
        return [
            pltpu.make_async_copy(k.at[:, cols(chip, head)], kb.at[head, slot(me)], local.at[0, head]),
            pltpu.make_async_copy(v.at[:, cols(chip, head)], vb.at[head, slot(me)], local.at[1, head]),
            pltpu.make_async_copy(q.at[:, cols(chip, head)], qb.at[head, chip], local.at[2, head]),
            pltpu.make_async_copy(tk.at[:, cols(chip, head)], tkb.at[head], tlocal.at[0, head]),
            pltpu.make_async_copy(tv.at[:, cols(chip, head)], tvb.at[head], tlocal.at[1, head]),
        ]

    def own_forward(head):
        return [
            across(
                src.at[:, cols(chip, head)], dst.at[head, slot(me)],
                fsend.at[index, head, 0], frecv.at[index, head, 0], {"seq": partner},
            )
            for index, (src, dst) in enumerate(((k, kb), (v, vb)))
        ]

    def forward(index, head, step):
        place = (kb, vb)[index].at[head, slot(chip_back(step) * CORES + core)]
        return across(
            place, place, fsend.at[index, head, step], frecv.at[index, head, step],
            {"seq": partner},
        )

    def count_copy(step):
        return across(
            counts, cb.at[me], csend.at[step - 1], crecv.at[step - 1],
            {"seq": lax.rem(me + step, n)},
        )

    def out_copy(head, step):
        target = chip_at(step)
        return across(
            ob.at[head, target], ab.at[c, t, head, chip],
            osend.at[head, step], orecv.at[head, step], {"seq": target * CORES + core},
        )

    def own_out(head):
        return pltpu.make_async_copy(
            ob.at[head, chip], ab.at[c, t, head, chip], orecv.at[head, 0]
        )

    def x_copy(head, index):
        place = ab.at[c, t, head, chip_back(index)]
        return across(place, place, xsend.at[head, index], xrecv.at[head, index], x_side)

    def y_copy(head, index):
        place = ab.at[c, t, head, chip_back(index)]
        return across(place, place, ysend.at[head, index], yrecv.at[head, index], y_side)

    def relay(head, index):
        if index % 2 == 0:
            place = ab.at[1 - c, t, head, chip_back(index)]
            side = x_side
        else:
            place = ab.at[c, 1 - t, head, chip_back(index)]
            side = y_side
        return across(place, place, rsend.at[head, index], rrecv.at[head, index], side)

    def w_own(head):
        return pltpu.make_async_copy(
            w.at[:, head, :, out_cols(t, c)], wb.at[head, t], wlocal.at[head]
        )

    def w_copy(head):
        part = pl.ds(core * half, half)
        return across(
            w.at[part, head, :, out_cols(1 - t, c)], wb.at[head, t, part],
            wsend.at[head], wrecv.at[head], x_side,
        )

    def w_forward(head):
        place = wb.at[head, 1 - t, pl.ds(core * half, half)]
        return across(place, place, wfsend.at[head], wfrecv.at[head], {"seq": partner})

    def stat_copy(step):
        return across(
            st, sg.at[me], ssend.at[step - 1], srecv.at[step - 1],
            {"seq": lax.rem(me + step, n)},
        )

    barrier = pltpu.get_barrier_semaphore()
    for step in range(1, n):
        pl.semaphore_signal(
            barrier, inc=1, device_id={"seq": lax.rem(me + step, n)}, device_id_type=MESH
        )
    pl.semaphore_signal(barrier, inc=1, device_id=x_side, device_id_type=MESH)
    pl.semaphore_signal(barrier, inc=1, device_id=y_side, device_id_type=MESH)

    def start_own(head, _):
        for copy in own_copies(head):
            copy.start()
        w_own(head).start()
        return 0

    lax.fori_loop(0, group, start_own, 0)
    pl.semaphore_wait(barrier, n + 1)

    def start_kv(head):
        for step in range(1, chips):
            for copy in kv_copies(head, step):
                copy.start()

    def start_q(head):
        for step in range(1, chips):
            q_copy(head, step).start()

    def start_first(head, _):
        start_kv(head)
        start_q(head)
        return 0

    for step in range(1, n):
        count_copy(step).start()
    lax.fori_loop(0, 2, start_first, 0)

    def start_near(head, _):
        w_copy(head).start()
        for copy in own_forward(head):
            copy.start()
        return 0

    lax.fori_loop(0, group, start_near, 0)

    cb[me] = counts[...]
    st[...] = jnp.zeros_like(st)
    for step in range(1, n):
        count_copy(step).wait_recv()
    lane = lax.broadcasted_iota(jnp.int32, (rows, HEAD_DIM), 1)
    place_in = lax.broadcasted_iota(jnp.int32, (rows, HEAD_DIM), 0)

    def fill_bias(source, _):
        limit = cb[source][0:1, :]
        bias[slot(source), :] = jnp.where(
            (lane == 0) & (place_in >= limit), NEGATIVE, 0.0
        ).astype(bf16)
        return 0

    lax.fori_loop(0, n, fill_bias, 0)
    tlane = lax.broadcasted_iota(jnp.int32, (text, HEAD_DIM), 1)
    tplace = lax.broadcasted_iota(jnp.int32, (text, HEAD_DIM), 0)
    tbias[...] = jnp.where(
        (tlane == 0) & (tplace >= lengths[0:1, :]), NEGATIVE, 0.0
    ).astype(bf16)

    total = n * rows
    size = chunk_rows(total, 768)

    def ones(length):
        return jnp.where(
            lax.broadcasted_iota(jnp.int32, (length, HEAD_DIM), 1) == 0, 1.0, 0.0
        ).astype(bf16)

    def one_block(head, target):
        query = jnp.concatenate([qb[head, target], ones(rows)], axis=1)

        def piece(state, keys, masks, vals):
            keys = jnp.concatenate([keys, masks], axis=1)
            vals = jnp.concatenate([vals, ones(vals.shape[0])], axis=1)
            scores = lax.dot_general(
                query, keys, (((1,), (1,)), ((), ())), preferred_element_type=f32
            )
            high = jnp.max(scores, axis=1, keepdims=True) * scale
            if state is not None:
                high = jnp.maximum(high, state[0])
            weights = jnp.exp2(scores * scale - high).astype(bf16)
            mixed = jnp.dot(weights, vals, preferred_element_type=f32)
            if state is not None:
                mixed = mixed + state[1] * jnp.exp2(state[0] - high)
            return (high, mixed)

        state = piece(None, tkb[head], tbias[...], tvb[head])
        for start in range(0, total, size):
            span = pl.ds(start, size)
            state = piece(state, kb[head, span], bias[span, :], vb[head, span])
        mixed = state[1]
        ob[head, target] = (
            mixed[:, :HEAD_DIM] / mixed[:, HEAD_DIM:HEAD_DIM + 1]
        ).astype(bf16)

    def take_keys(head):
        for copy in own_copies(head):
            copy.wait()
        for step in range(1, chips):
            made = kv_copies(head, step)
            for index in range(2):
                made[index].wait_recv()
                forward(index, head, step).start()
        for copy in own_forward(head):
            copy.wait_recv()
        for step in range(1, chips):
            for index in range(2):
                forward(index, head, step).wait_recv()

    def blocks(head, between):
        def block(step, _):
            far = step < chips

            @pl.when(far)
            def _():
                q_copy(head, step).wait_recv()

            one_block(head, chip_back(step))

            @pl.when(far)
            def _():
                out_copy(head, chips - step).start()

            @pl.when(step == chips)
            def _():
                own_out(head).start()

            if between is not None:
                @pl.when(step == 2)
                def _():
                    between()
            return 0

        lax.fori_loop(1, chips + 1, block, 0)

    def share(head):
        for index in (0, *range(chips - 1, 0, -1)):
            if index == 0:
                own_out(head).wait()
            else:
                out_copy(head, index).wait_recv()
            x_copy(head, index).start()
            y_copy(head, index).start()

    def pass_on(head):
        for index in (0, *range(chips - 1, 0, -1)):
            (x_copy if index % 2 else y_copy)(head, index).wait_recv()
            relay(head, index).start()

    def collect(head):
        for index in range(chips):
            (y_copy if index % 2 else x_copy)(head, index).wait_recv()
        for index in range(chips):
            relay(head, index).wait_recv()
        w_own(head).wait()
        w_forward(head).wait_recv()

    part = 256 if wide % 256 == 0 else HEAD_DIM
    depth = CORES * chips * HEAD_DIM

    def product(head, branch, span):
        rows_in = jnp.concatenate(
            [ab[branch, side, head, source] for side in range(2) for source in range(chips)],
            axis=1,
        )
        weight = wb[head, :, :, :, span].reshape(depth, part)
        return jnp.dot(rows_in, weight, preferred_element_type=f32)

    def span_of(index):
        return pl.ds(pl.multiple_of(index * part, HEAD_DIM), part)

    def project(head):
        def one(index, _):
            span = span_of(index)
            for branch in range(2):
                acc[branch, :, span] += product(head, branch, span)
            return 0

        lax.fori_loop(0, wide // part, one, 0)

    acc[...] = jnp.zeros_like(acc)

    def one_head(head, _):
        take_keys(head)
        blocks(head, None)

        @pl.when(head + 2 < group)
        def _():
            start_kv(head + 2)

        @pl.when(head + 2 < last)
        def _():
            start_q(head + 2)

        @pl.when(head + 1 == last)
        def _():
            start_q(last)

        @pl.when(head == 1)
        def _():
            def pass_weight(index, _):
                w_copy(index).wait_recv()
                w_forward(index).start()
                return 0

            lax.fori_loop(0, group, pass_weight, 0)

        @pl.when(head >= 1)
        def _():
            share(head - 1)
            pass_on(head - 1)
            collect(head - 1)
            project(head - 1)

        return 0

    lax.fori_loop(0, last, one_head, 0)
    take_keys(last)
    share(last - 1)
    blocks(last, lambda: pass_on(last - 1))
    share(last)
    collect(last - 1)
    project(last - 1)
    pass_on(last)
    collect(last)

    limit = counts[0:1, 0:1]
    valid = lax.broadcasted_iota(jnp.int32, (rows, part), 0) < limit

    def guide(index, _):
        span = span_of(index)
        conditional, unconditional = [
            (acc[branch, :, span] + product(last, branch, span)).astype(bf16).astype(f32)
            for branch in range(2)
        ]
        guided = unconditional + GUIDANCE * (conditional - unconditional)
        acc[0, :, span] = guided
        guided = jnp.where(valid, guided, 0.0)
        conditional = jnp.where(valid, conditional, 0.0)
        for row, field in enumerate(
            (guided, guided * guided, conditional, conditional * conditional)
        ):
            st[row:row + 1, span] = jnp.sum(field, axis=0, keepdims=True)
        st[4:5, span] = jnp.broadcast_to(limit.astype(f32), (1, part))
        return 0

    lax.fori_loop(0, wide // part, guide, 0)

    for step in range(1, n):
        stat_copy(step).start()
    sg[me] = st[...]

    def settle(head, _):
        for step in range(1, chips):
            for copy in kv_copies(head, step):
                copy.wait_send()
            q_copy(head, step).wait_send()
            out_copy(head, step).wait_send()
            for index in range(2):
                forward(index, head, step).wait_send()
        for copy in own_forward(head):
            copy.wait_send()
        for index in range(chips):
            x_copy(head, index).wait_send()
            y_copy(head, index).wait_send()
            relay(head, index).wait_send()
        w_copy(head).wait_send()
        w_forward(head).wait_send()
        return 0

    lax.fori_loop(0, group, settle, 0)
    for step in range(1, n):
        count_copy(step).wait_send()
    for step in range(1, n):
        stat_copy(step).wait()
    sums = sg[0]
    for source in range(1, n):
        sums = sums + sg[source]
    st[...] = sums

    def finish(index, _):
        span = span_of(index)
        here = st[:, span]
        valid_total = here[4:5, :]
        guided_mean = here[0:1, :] / valid_total
        guided_var = here[1:2, :] / valid_total - guided_mean * guided_mean
        cond_mean = here[2:3, :] / valid_total
        cond_var = here[3:4, :] / valid_total - cond_mean * cond_mean
        std_ratio = jnp.sqrt((cond_var + 1.0) / (guided_var + 1.0))
        factor = RESCALE * std_ratio + (1.0 - RESCALE)
        out[:, span] = (guided_mean + (acc[0, :, span] - guided_mean) * factor).astype(bf16)
        return 0

    lax.fori_loop(0, wide // part, finish, 0)


def fused_step(
    queries, keys, values, text_keys, text_values, prompt_lengths, frame_counts, out_weight, n
):
    rows, width = queries.shape
    text = text_keys.shape[0]
    chips = n // CORES
    heads = width // HEAD_DIM
    group = heads // chips
    wide = out_weight.shape[1] // 4
    counts = jnp.broadcast_to(frame_counts.reshape(1, 1), (8, HEAD_DIM))
    lengths = jnp.broadcast_to(prompt_lengths.reshape(1, 1), (8, HEAD_DIM))
    weight = out_weight.reshape(chips, group, HEAD_DIM, out_weight.shape[1])
    bf16 = jnp.bfloat16
    f32 = jnp.float32
    total = n * rows
    hbm = pl.BlockSpec(memory_space=pl.ANY)
    vmem = pl.BlockSpec(memory_space=pltpu.VMEM)
    dma = pltpu.SemaphoreType.DMA
    return pl.pallas_call(
        functools.partial(step_kernel, n, chips, group, rows, text, wide),
        out_shape=jax.ShapeDtypeStruct((rows, wide), bf16),
        in_specs=[hbm] * 6 + [vmem] * 2,
        out_specs=vmem,
        scratch_shapes=[
            pltpu.VMEM((group, chips, rows, HEAD_DIM), bf16),
            pltpu.VMEM((group, total, HEAD_DIM), bf16),
            pltpu.VMEM((group, total, HEAD_DIM), bf16),
            pltpu.VMEM((group, text, HEAD_DIM), bf16),
            pltpu.VMEM((group, text, HEAD_DIM), bf16),
            pltpu.VMEM((n, 8, HEAD_DIM), jnp.int32),
            pltpu.VMEM((total, HEAD_DIM), bf16),
            pltpu.VMEM((text, HEAD_DIM), bf16),
            pltpu.VMEM((group, chips, rows, HEAD_DIM), bf16),
            pltpu.VMEM((2, 2, group, chips, rows, HEAD_DIM), bf16),
            pltpu.VMEM((group, 2, chips, HEAD_DIM, wide), bf16),
            pltpu.VMEM((2, rows, wide), f32),
            pltpu.VMEM((8, wide), f32),
            pltpu.VMEM((n, 8, wide), f32),
            dma((3, group, chips - 1)),
            dma((3, group, chips - 1)),
            dma((2, group, chips)),
            dma((2, group, chips)),
            dma((n - 1,)),
            dma((n - 1,)),
            dma((3, group)),
            dma((2, group)),
            dma((group, chips)),
            dma((group, chips)),
            dma((group, chips)),
            dma((group, chips)),
            dma((group, chips)),
            dma((group, chips)),
            dma((group, chips)),
            dma((group, chips)),
            dma((group,)),
            dma((group,)),
            dma((group,)),
            dma((group,)),
            dma((group,)),
            dma((n - 1,)),
            dma((n - 1,)),
        ],
        compiler_params=pltpu.CompilerParams(
            collective_id=0, has_side_effects=True, vmem_limit_bytes=62 * 1024 * 1024
        ),
    )(queries, keys, values, text_keys, text_values, weight, counts, lengths)


def frame_valid(positions, counts_table, slots):
    frame_index = positions // slots
    slot_index = positions % slots
    frame_ids = jnp.arange(counts_table.shape[0], dtype=jnp.int32)
    frame_limit = jnp.sum(
        jnp.where(frame_index[:, None] == frame_ids[None, :], counts_table[None, :], 0), axis=1
    )
    return slot_index < frame_limit


def attend_block(carry, key_rows, value_rows, query_heads, key_mask):
    row_max, weight_sum, mixed_sum = carry
    head_count = query_heads.shape[1]
    key_heads = key_rows.reshape(key_rows.shape[0], head_count, HEAD_DIM)
    value_heads = value_rows.reshape(value_rows.shape[0], head_count, HEAD_DIM)
    scores = jnp.einsum(
        "qhd,khd->hqk", query_heads, key_heads, preferred_element_type=jnp.float32
    ) * HEAD_DIM ** (-0.5)
    scores = jnp.where(key_mask[None, None, :], scores, NEGATIVE)
    new_max = jnp.maximum(row_max, jnp.max(scores, axis=2))
    shrink = jnp.exp(row_max - new_max)
    weights = jnp.exp(scores - new_max[:, :, None])
    weight_sum = weight_sum * shrink + jnp.sum(weights, axis=2)
    mixed_sum = mixed_sum * shrink[:, :, None] + jnp.einsum(
        "hqk,khd->hqd",
        weights.astype(jnp.bfloat16),
        value_heads,
        preferred_element_type=jnp.float32,
    )
    return (new_max, weight_sum, mixed_sum)


def gathered_attention(
    queries, keys, values, text_keys, text_values, prompt_lengths, frame_counts, n
):
    row_count, head_cols = queries.shape
    head_count = head_cols // HEAD_DIM
    all_counts = lax.all_gather(frame_counts, "seq", axis=0, tiled=True)
    query_heads = queries.reshape(row_count, head_count, HEAD_DIM)
    text_mask = jnp.arange(text_keys.shape[0], dtype=jnp.int32) < prompt_lengths[0]
    empty_state = (
        jnp.full((head_count, row_count), NEGATIVE, jnp.float32),
        jnp.zeros((head_count, row_count), jnp.float32),
        jnp.zeros((head_count, row_count, HEAD_DIM), jnp.float32),
    )
    text_state = attend_block(empty_state, text_keys, text_values, query_heads, text_mask)
    key_rows = lax.all_gather(keys, "seq", axis=0, tiled=True)
    value_rows = lax.all_gather(values, "seq", axis=0, tiled=True)
    positions = jnp.arange(key_rows.shape[0], dtype=jnp.int32)
    _, weight_sum, mixed_sum = attend_block(
        text_state, key_rows, value_rows, query_heads,
        frame_valid(positions, all_counts, row_count // frame_counts.shape[0]),
    )
    return (
        jnp.transpose(mixed_sum / weight_sum[:, :, None], (1, 0, 2))
        .reshape(row_count, head_cols)
        .astype(jnp.bfloat16)
    )


def fits_fused(n, cfgs, tps, queries, frame_counts, out_weight):
    heads = queries.shape[2] // HEAD_DIM
    chips = n // CORES
    if cfgs != 2 or tps != 2 or n % CORES or frame_counts.shape[0] != 1:
        return False
    if chips < 2 or chips % 2 or heads % chips or heads // chips < 3:
        return False
    return out_weight.shape[1] % (4 * HEAD_DIM) == 0 and queries.shape[1] % 16 == 0


def body(n, cfgs, tps, queries, keys, values, text_keys, text_values, prompt_lengths, frame_counts, out_weight):
    rows = queries.shape[1]
    if fits_fused(n, cfgs, tps, queries, frame_counts, out_weight):
        return fused_step(
            queries[0], keys[0], values[0], text_keys[0], text_values[0],
            prompt_lengths, frame_counts, out_weight, n,
        )
    attended = gathered_attention(
        queries[0], keys[0], values[0], text_keys[0], text_values[0],
        prompt_lengths, frame_counts, n,
    )
    branch = lax.psum_scatter(
        lax.dot_general(
            out_weight, attended, (((0,), (1,)), ((), ())), preferred_element_type=jnp.float32
        ).astype(jnp.bfloat16),
        "tp",
        scatter_dimension=0,
        tiled=True,
    )
    half = branch.shape[0] // cfgs
    mine = lax.axis_index("cfg")
    kept = lax.dynamic_slice_in_dim(branch, mine * half, half, 0)
    given = lax.dynamic_slice_in_dim(branch, (1 - mine) * half, half, 0)
    other = lax.ppermute(given, "cfg", [(0, 1), (1, 0)])
    first = mine == 0
    conditional = jnp.where(first, kept, other).astype(jnp.float32)
    unconditional = jnp.where(first, other, kept).astype(jnp.float32)
    guided = unconditional + GUIDANCE * (conditional - unconditional)
    valid = (jnp.arange(rows, dtype=jnp.int32) < frame_counts[0])[None, :]

    def local_sum(field):
        return jnp.sum(jnp.where(valid, field, 0.0), axis=1)

    sums = lax.psum(
        jnp.stack([
            local_sum(guided),
            local_sum(guided * guided),
            local_sum(conditional),
            local_sum(conditional * conditional),
            jnp.full((half,), frame_counts[0].astype(jnp.float32)),
        ]),
        "seq",
    )
    means = sums[:4] / sums[4:5]
    guided_mean = means[0]
    guided_var = means[1] - guided_mean * guided_mean
    cond_var = means[3] - means[2] * means[2]
    std_ratio = jnp.sqrt((cond_var + 1.0) / (guided_var + 1.0))
    factor = RESCALE * std_ratio + (1.0 - RESCALE)
    velocity = guided_mean[:, None] + (guided - guided_mean[:, None]) * factor[:, None]
    return velocity.astype(jnp.bfloat16).T


def solution(mesh):
    placed = (
        P("cfg", "seq", "tp"),
        P("cfg", "seq", "tp"),
        P("cfg", "seq", "tp"),
        P("cfg", None, "tp"),
        P("cfg", None, "tp"),
        P("cfg"),
        P("seq"),
        P("tp", None),
    )
    return jax.shard_map(
        functools.partial(body, mesh.shape["seq"], mesh.shape["cfg"], mesh.shape["tp"]),
        mesh=mesh, in_specs=placed, out_specs=P("seq", ("tp", "cfg")), check_vma=False,
    )
```

time: 294 us -> 266 us (0.905)
  Pallas kernels: 289 us -> 261 us
    pallas_call x2 -> x1, Pallas kernels: 289 us -> 261 us  [fused_step(): pl.pallas_call(functools.partial(step_kernel, n, chips, group, rows, text...]
where the time goes in v1:
time: 266 us; the launch traced here: 265 us
  Pallas kernels  261 us (98%)
  local copies, waits for them, and re-layouts  3.58 us (1%)
    pallas_call x1, Pallas kernels, fused_step(): pl.pallas_call(functools.partial(step_kernel, n, chips, group, rows, text...  261 us

profile of v1, /device:TPU:0, one launch (start us, length us, event | category | flops | bytes accessed | tf_op | source)
XLA Modules:
  0.0 265.4 jit_solution(13176826609666770685)
XLA Ops:
  1.3 0.6 broadcast_in_dim.17.lengths
  1.9 0.6 broadcast_in_dim.15.counts
  2.5 260.5 %shard_map.82 = bf16[480,1280]{1,0:T(8,128)(2,1)} custom-call(bf16[480,2560]{1,0:T(8,128)(2,1)} %bitcast.13, bf16[480,2560]{1,0:T(8,128)(2,1)} %bitcast.14, bf16[480,2560]{1,0:T(8,128)(2,1)} %bitcast.15, bf16[512,2560]{1,0:T(8,128)(2,1)} %bitcast.11, bf16[512,2560]{1,0:T(8,128)(2,1)} %bitcast.12, bf16[4,5,128,5120]{3,2,1,0:T(8,128)(2,1)} %bitcast.10, ...), custom_call_target="tpu_custom_call" | custom-call | tf_op jit(solution)/shard_map/pallas_call | solution.py:491
  263.0 2.4 copy.12

commit v2 on v1

v2 whole, which is shorter than its diff:
```python
import functools

import jax
import jax.numpy as jnp
from jax import lax
from jax.experimental import pallas as pl
from jax.experimental.pallas import tpu as pltpu
from jax.sharding import PartitionSpec as P

HEAD_DIM = 128
GUIDANCE = 5.0
RESCALE = 0.7
NEGATIVE = -1e30
LOG2E = 1.4426950408889634
CORES = 2
MESH = pl.DeviceIdType.MESH


def chunk_rows(total, limit):
    for unit in (256, 128, 16):
        for size in range(limit // unit * unit, 0, -unit):
            if total % size == 0:
                return size
    return total


def step_kernel(
    n, chips, group, rows, text, wide, part,
    q, k, v, tk, tv, w, counts, lengths,
    out,
    qb, kb, vb, tkb, tvb, mc, cb, bias, tbias, ob, ab, wb, acc, st, sg, vel,
    send, krecv, qrecv, frecv, count, local, orecv, passed, direct, relayed, wsem, stat, vsem,
):
    me = lax.axis_index("seq")
    t = lax.axis_index("tp")
    c = lax.axis_index("cfg")
    core = lax.rem(me, CORES)
    chip = lax.div(me, CORES)
    partner = chip * CORES + (CORES - 1 - core)
    scale = LOG2E * HEAD_DIM ** (-0.5)
    last = group - 1
    half = chips // 2
    bf16 = jnp.bfloat16
    f32 = jnp.float32

    def cols(owner, head):
        return pl.ds(pl.multiple_of((owner * group + head) * HEAD_DIM, HEAD_DIM), HEAD_DIM)

    def out_cols(side, branch):
        return pl.ds(pl.multiple_of((side * 2 + branch) * wide, HEAD_DIM), wide)

    def slot(index):
        return pl.ds(pl.multiple_of(index * rows, 16), rows)

    def chip_at(step):
        return lax.rem(chip + step, chips)

    mid = chips // 2
    late = mid - lax.div(chip, mid)
    gap = lax.rem(chip + chips - late, chips)
    at_end = lax.rem(chip, chips - 1) == 0
    inside = lax.rem(chip, chips - 1) != 0

    def source(place):
        other = lax.rem(late + place + lax.div(place + chips - gap, chips), chips)
        return jnp.where(place == 0, chip, other)

    def step_from(other):
        return lax.rem(chip + chips - other, chips)

    def step_to(other):
        return lax.rem(other + chips - chip, chips)

    def chip_back(step):
        return lax.rem(chip + chips - step, chips)

    def across(src, dst, sends, recvs, device):
        return pltpu.make_async_remote_copy(
            src_ref=src, dst_ref=dst, send_sem=sends, recv_sem=recvs,
            device_id=device, device_id_type=MESH,
        )

    def drain(ref, sem):
        pltpu.make_async_copy(ref, ref, sem).wait()

    def blocks_of(number):
        return kb.at[0, pl.ds(0, number * rows)]

    x_side = {"tp": 1 - t}
    y_side = {"cfg": 1 - c}

    def kv_copies(head, step):
        target = chip_at(step)
        return [
            across(
                src.at[:, cols(target, head)], dst.at[head, slot(me)],
                send.at[head], krecv.at[head, step - 1], {"seq": target * CORES + core},
            )
            for src, dst in ((k, kb), (v, vb))
        ]

    def q_copy(head, step):
        target = chip_at(step)
        return across(
            q.at[:, cols(target, head)], qb.at[head, chip],
            send.at[head], qrecv.at[head, step - 1], {"seq": target * CORES + core},
        )

    def own_copies(head):
        return [
            pltpu.make_async_copy(k.at[:, cols(chip, head)], kb.at[head, slot(me)], local.at[head]),
            pltpu.make_async_copy(v.at[:, cols(chip, head)], vb.at[head, slot(me)], local.at[head]),
            pltpu.make_async_copy(q.at[:, cols(chip, head)], qb.at[head, chip], local.at[head]),
            pltpu.make_async_copy(tk.at[:, cols(chip, head)], tkb.at[head], local.at[head]),
            pltpu.make_async_copy(tv.at[:, cols(chip, head)], tvb.at[head], local.at[head]),
        ]

    def own_forward(head):
        return [
            across(
                src.at[:, cols(chip, head)], dst.at[head, slot(me)],
                send.at[head], frecv.at[head], {"seq": partner},
            )
            for src, dst in ((k, kb), (v, vb))
        ]

    def forwards(head, step):
        span = slot(chip_back(step) * CORES + core)
        return [
            across(
                buf.at[head, span], buf.at[head, span], send.at[head], frecv.at[head],
                {"seq": partner},
            )
            for buf in (kb, vb)
        ]

    def count_copy(step):
        return across(
            mc, cb.at[me], count.at[0], count.at[1],
            {"seq": lax.rem(me + step, n)},
        )

    def out_copy(head, step):
        target = chip_at(step)
        return across(
            ob.at[head, target], ab.at[c, t, head, chip],
            send.at[head], orecv.at[head, step], {"seq": target * CORES + core},
        )

    def own_out(head):
        return pltpu.make_async_copy(
            ob.at[head, chip], ab.at[c, t, head, chip], orecv.at[head, 0]
        )

    def arrived(head, place, odd):
        if place % 2 == odd:
            return passed.at[head, place // (chips - 1)]
        return direct.at[head]

    def x_copy(head, place):
        piece = ab.at[c, t, head, source(place)]
        return across(piece, piece, send.at[head], arrived(head, place, 1), x_side)

    def y_copy(head, place):
        piece = ab.at[c, t, head, source(place)]
        return across(piece, piece, send.at[head], arrived(head, place, 0), y_side)

    def relay(head, place):
        if place % 2 == 0:
            piece = ab.at[1 - c, t, head, source(place)]
            side = x_side
        else:
            piece = ab.at[c, 1 - t, head, source(place)]
            side = y_side
        return across(piece, piece, send.at[head], relayed.at[head], side)

    def w_own(head):
        return pltpu.make_async_copy(
            w.at[:, head, :, out_cols(t, c)], wb.at[head, t], wsem.at[0]
        )

    def w_copy(head):
        part = pl.ds(core * half, half)
        return across(
            w.at[part, head, :, out_cols(1 - t, c)], wb.at[head, t, part],
            wsem.at[3], wsem.at[1], x_side,
        )

    def w_forward(head):
        place = wb.at[head, 1 - t, pl.ds(core * half, half)]
        return across(place, place, wsem.at[3], wsem.at[2], {"seq": partner})

    parts = wide // part

    def stat_copy(turn, step):
        span = (pl.ds(0, parts - 1), pl.ds(parts - 1, 1))[turn]
        return across(
            st.at[span], sg.at[me, span], stat.at[0], stat.at[1],
            {"seq": lax.rem(me + step, n)},
        )

    mc[...] = jnp.full(mc.shape, counts[0], jnp.int32)
    barrier = pltpu.get_barrier_semaphore()
    for step in range(1, n):
        pl.semaphore_signal(
            barrier, inc=1, device_id={"seq": lax.rem(me + step, n)}, device_id_type=MESH
        )
    pl.semaphore_signal(barrier, inc=1, device_id=x_side, device_id_type=MESH)
    pl.semaphore_signal(barrier, inc=1, device_id=y_side, device_id_type=MESH)

    def start_own(head, _):
        for copy in own_copies(head):
            copy.start()
        w_own(head).start()
        return 0

    lax.fori_loop(0, group, start_own, 0)
    pl.semaphore_wait(barrier, n + 1)

    def start_kv(head):
        for step in range(1, chips):
            for copy in kv_copies(head, step):
                copy.start()

    def start_q(head):
        for step in range(1, chips):
            q_copy(head, step).start()

    for step in range(1, n):
        count_copy(step).start()
    start_kv(0)
    start_q(0)

    @pl.when(inside)
    def _():
        start_kv(1)


    def start_near(head, _):
        w_copy(head).start()
        for copy in own_forward(head):
            copy.start()
        return 0

    lax.fori_loop(0, group, start_near, 0)

    cb[me] = mc[...]
    st[...] = jnp.zeros_like(st)
    acc[...] = jnp.zeros_like(acc)
    drain(cb.at[pl.ds(0, n - 1)], count.at[1])
    lane = lax.broadcasted_iota(jnp.int32, (rows, HEAD_DIM), 1)
    place_in = lax.broadcasted_iota(jnp.int32, (rows, HEAD_DIM), 0)

    def fill_bias(source, _):
        limit = cb[source][0:1, :]
        bias[slot(source), :] = jnp.where(
            (lane == 0) & (place_in >= limit), NEGATIVE, 0.0
        ).astype(bf16)
        return 0

    lax.fori_loop(0, n, fill_bias, 0)
    tlane = lax.broadcasted_iota(jnp.int32, (text, HEAD_DIM), 1)
    tplace = lax.broadcasted_iota(jnp.int32, (text, HEAD_DIM), 0)
    tbias[...] = jnp.where(
        (tlane == 0) & (tplace >= lengths[0]), NEGATIVE, 0.0
    ).astype(bf16)

    total = n * rows
    size = chunk_rows(total, 768)

    def ones(length):
        return jnp.where(
            lax.broadcasted_iota(jnp.int32, (length, HEAD_DIM), 1) == 0, 1.0, 0.0
        ).astype(bf16)

    def one_block(head, target):
        query = jnp.concatenate([qb[head, target], ones(rows)], axis=1)

        def piece(state, keys, masks, vals):
            keys = jnp.concatenate([keys, masks], axis=1)
            vals = jnp.concatenate([vals, ones(vals.shape[0])], axis=1)
            scores = lax.dot_general(
                query, keys, (((1,), (1,)), ((), ())), preferred_element_type=f32
            )
            high = jnp.max(scores, axis=1, keepdims=True) * scale
            if state is not None:
                high = jnp.maximum(high, state[0])
            weights = jnp.exp2(scores * scale - high).astype(bf16)
            mixed = jnp.dot(weights, vals, preferred_element_type=f32)
            if state is not None:
                mixed = mixed + state[1] * jnp.exp2(state[0] - high)
            return (high, mixed)

        state = piece(None, tkb[head], tbias[...], tvb[head])
        for start in range(0, total, size):
            span = pl.ds(start, size)
            state = piece(state, kb[head, span], bias[span, :], vb[head, span])
        mixed = state[1]
        ob[head, target] = (
            mixed[:, :HEAD_DIM] / mixed[:, HEAD_DIM:HEAD_DIM + 1]
        ).astype(bf16)

    def take_keys(head):
        drain(kb.at[0, pl.ds(0, 3 * rows + 2 * text)], local.at[head])
        for step in range(1, chips):
            drain(blocks_of(2), krecv.at[head, step - 1])
            for copy in forwards(head, step):
                copy.start()
        drain(blocks_of(n), frecv.at[head])

    def share_piece(head, place):
        if place == 0:
            own_out(head).wait()
        else:
            out_copy(head, step_from(source(place))).wait_recv()
        x_copy(head, place).start()
        y_copy(head, place).start()

    def share(head, places):
        for place in places:
            share_piece(head, place)

    def pass_early(head):
        drain(blocks_of(chips - 1), passed.at[head, 0])
        for place in range(chips - 1):
            relay(head, place).start()

    def pass_late(head):
        drain(blocks_of(1), passed.at[head, 1])
        relay(head, chips - 1).start()

    def blocks(head, after):
        def block(place, _):
            other = source(place)
            far = place > 0

            @pl.when(far)
            def _():
                q_copy(head, step_from(other)).wait_recv()

            if after is None:
                @pl.when((place == chips - 1) & at_end)
                def _():
                    start_kv(head + 1)

            one_block(head, other)

            @pl.when(far)
            def _():
                out_copy(head, step_to(other)).start()

            @pl.when(place == 0)
            def _():
                own_out(head).start()
                share_piece(head, 0)

            if after is not None:
                after(place)
            return 0

        lax.fori_loop(0, chips, block, 0)

    def collect_direct(head):
        drain(blocks_of(chips), direct.at[head])

    def collect_relayed(head):
        drain(blocks_of(chips), relayed.at[head])

    def collect(head):
        collect_direct(head)
        collect_relayed(head)

    depth = 2 * chips * HEAD_DIM

    def product(head, branch, span):
        rows_in = jnp.concatenate(
            [ab[branch, side, head, source] for side in range(2) for source in range(chips)],
            axis=1,
        )
        weight = wb[head, :, :, :, span].reshape(depth, part)
        return jnp.dot(rows_in, weight, preferred_element_type=f32)

    def side_product(head, branch, side, span):
        rows_in = jnp.concatenate(
            [ab[branch, side, head, source] for source in range(chips)], axis=1
        )
        weight = wb[head, side, :, :, span].reshape(chips * HEAD_DIM, part)
        return jnp.dot(rows_in, weight, preferred_element_type=f32)

    def span_of(index):
        return pl.ds(pl.multiple_of(index * part, HEAD_DIM), part)

    def project(head):
        def one(index, _):
            span = span_of(index)
            for branch in range(2):
                acc[branch, :, span] += product(head, branch, span)
            return 0

        lax.fori_loop(0, parts, one, 0)

    def project_side(head, branch, side):
        def one(index, _):
            span = span_of(index)
            acc[branch, :, span] += side_product(head, branch, side, span)
            return 0

        lax.fori_loop(0, parts, one, 0)

    near = pl.ds(0, half)

    def pass_weight(index, _):
        w_forward(index).start()
        return 0

    def one_head(head, _):
        take_keys(head)
        blocks(head, None)
        start_q(head + 1)

        @pl.when(inside & (head + 2 <= last))
        def _():
            start_kv(head + 2)

        @pl.when(head == 1)
        def _():
            drain(wb.at[:, 0, near], wsem.at[1])
            lax.fori_loop(0, group, pass_weight, 0)

        @pl.when(head >= 1)
        def _():
            pass_early(head - 1)
            pass_late(head - 1)

        @pl.when(head + 1 < last)
        def _():
            share(head, range(1, chips))

        @pl.when(head == 1)
        def _():
            drain(wb.at[:, 0], wsem.at[0])
            drain(wb.at[:, 0, near], wsem.at[2])

        @pl.when(head >= 1)
        def _():
            collect(head - 1)
            project(head - 1)

        return 0

    lax.fori_loop(0, last, one_head, 0)
    share(last - 1, range(1, chips - 1))
    take_keys(last)

    def after_block(place):
        @pl.when(place == 0)
        def _():
            share_piece(last - 1, chips - 1)
            pass_early(last - 1)

        @pl.when(place == chips - 2)
        def _():
            pass_late(last - 1)

    blocks(last, after_block)
    collect(last - 1)
    project(last - 1)
    share(last, range(1, chips))
    project_side(last, c, t)
    pass_early(last)
    pass_late(last)
    collect_direct(last)
    project_side(last, c, 1 - t)
    project_side(last, 1 - c, t)
    collect_relayed(last)

    limit = cb[me][0:1, 0:1]
    valid = lax.broadcasted_iota(jnp.int32, (rows, part), 0) < limit
    first = jnp.full((rows, part), c, jnp.int32) == 0
    pairs = part // HEAD_DIM

    def guide(index, _):
        span = span_of(index)
        mine = acc[c, :, span].astype(bf16).astype(f32)
        other = acc[1 - c, :, span] + side_product(last, 1 - c, 1 - t, span)
        other = other.astype(bf16).astype(f32)
        conditional = jnp.where(first, mine, other)
        unconditional = jnp.where(first, other, mine)
        guided = unconditional + GUIDANCE * (conditional - unconditional)
        acc[0, :, span] = guided
        guided = jnp.where(valid, guided, 0.0)
        conditional = jnp.where(valid, conditional, 0.0)
        for row, field in enumerate(
            (guided, guided * guided, conditional, conditional * conditional)
        ):
            total_row = jnp.sum(field, axis=0, keepdims=True)
            for pair in range(pairs):
                st[index, 4 * pair + row:4 * pair + row + 1, :] = total_row[
                    :, pair * HEAD_DIM:(pair + 1) * HEAD_DIM
                ]

        @pl.when(index == parts - 2)
        def _():
            for step in range(1, n):
                stat_copy(0, step).start()

        return 0

    lax.fori_loop(0, parts, guide, 0)
    for step in range(1, n):
        stat_copy(1, step).start()

    def settle(head, _):
        drain(kb.at[pl.ds(0, chips)], send.at[head])
        return 0

    lax.fori_loop(0, group, settle, 0)
    drain(wb.at[:, 0], wsem.at[3])
    drain(cb.at[pl.ds(0, n - 1)], count.at[0])
    valid_total = cb[0][0:1, :]
    for source in range(1, n):
        valid_total = valid_total + cb[source][0:1, :]
    valid_total = valid_total.astype(f32)

    def store(index):
        return pltpu.make_async_copy(vel.at[index], out.at[:, span_of(index)], vsem.at[0])

    drain(sg.at[pl.ds(0, n - 1)], stat.at[1])

    def finish(index, _):
        sums = st[index]
        for step in range(1, n):
            sums = sums + sg[lax.rem(me + step, n), index]
        for pair in range(pairs):
            here = sums[4 * pair:4 * pair + 4] / valid_total
            guided_mean = here[0:1, :]
            guided_var = here[1:2, :] - guided_mean * guided_mean
            cond_mean = here[2:3, :]
            cond_var = here[3:4, :] - cond_mean * cond_mean
            std_ratio = jnp.sqrt((cond_var + 1.0) / (guided_var + 1.0))
            factor = RESCALE * std_ratio + (1.0 - RESCALE)
            span = pl.ds(pl.multiple_of(index * part + pair * HEAD_DIM, HEAD_DIM), HEAD_DIM)
            vel[index, :, pair * HEAD_DIM:(pair + 1) * HEAD_DIM] = (
                guided_mean + (acc[0, :, span] - guided_mean) * factor
            ).astype(bf16)
        store(index).start()
        return 0

    lax.fori_loop(0, parts, finish, 0)

    drain(sg.at[pl.ds(0, n - 1)], stat.at[0])
    drain(vel, vsem.at[0])


def fused_step(
    queries, keys, values, text_keys, text_values, prompt_lengths, frame_counts, out_weight, n
):
    rows, width = queries.shape
    text = text_keys.shape[0]
    chips = n // CORES
    heads = width // HEAD_DIM
    group = heads // chips
    wide = out_weight.shape[1] // 4
    part = 256 if wide % 256 == 0 else HEAD_DIM
    parts = wide // part
    weight = out_weight.reshape(chips, group, HEAD_DIM, out_weight.shape[1])
    bf16 = jnp.bfloat16
    f32 = jnp.float32
    total = n * rows
    hbm = pl.BlockSpec(memory_space=pl.ANY)
    smem = pl.BlockSpec(memory_space=pltpu.SMEM)
    dma = pltpu.SemaphoreType.DMA
    return pl.pallas_call(
        functools.partial(step_kernel, n, chips, group, rows, text, wide, part),
        out_shape=jax.ShapeDtypeStruct((rows, wide), bf16),
        in_specs=[hbm] * 6 + [smem] * 2,
        out_specs=hbm,
        scratch_shapes=[
            pltpu.VMEM((group, chips, rows, HEAD_DIM), bf16),
            pltpu.VMEM((group, total, HEAD_DIM), bf16),
            pltpu.VMEM((group, total, HEAD_DIM), bf16),
            pltpu.VMEM((group, text, HEAD_DIM), bf16),
            pltpu.VMEM((group, text, HEAD_DIM), bf16),
            pltpu.VMEM((8, HEAD_DIM), jnp.int32),
            pltpu.VMEM((n, 8, HEAD_DIM), jnp.int32),
            pltpu.VMEM((total, HEAD_DIM), bf16),
            pltpu.VMEM((text, HEAD_DIM), bf16),
            pltpu.VMEM((group, chips, rows, HEAD_DIM), bf16),
            pltpu.VMEM((2, 2, group, chips, rows, HEAD_DIM), bf16),
            pltpu.VMEM((group, 2, chips, HEAD_DIM, wide), bf16),
            pltpu.VMEM((2, rows, wide), f32),
            pltpu.VMEM((parts, 8, HEAD_DIM), f32),
            pltpu.VMEM((n, parts, 8, HEAD_DIM), f32),
            pltpu.VMEM((parts, rows, part), bf16),
            dma((group,)),
            dma((group, chips - 1)),
            dma((group, chips - 1)),
            dma((group,)),
            dma((2,)),
            dma((group,)),
            dma((group, chips)),
            dma((group, 2)),
            dma((group,)),
            dma((group,)),
            dma((4,)),
            dma((2,)),
            dma((1,)),
        ],
        compiler_params=pltpu.CompilerParams(
            collective_id=0, has_side_effects=True, vmem_limit_bytes=62 * 1024 * 1024
        ),
    )(queries, keys, values, text_keys, text_values, weight, frame_counts, prompt_lengths)


def frame_valid(positions, counts_table, slots):
    frame_index = positions // slots
    slot_index = positions % slots
    frame_ids = jnp.arange(counts_table.shape[0], dtype=jnp.int32)
    frame_limit = jnp.sum(
        jnp.where(frame_index[:, None] == frame_ids[None, :], counts_table[None, :], 0), axis=1
    )
    return slot_index < frame_limit


def attend_block(carry, key_rows, value_rows, query_heads, key_mask):
    row_max, weight_sum, mixed_sum = carry
    head_count = query_heads.shape[1]
    key_heads = key_rows.reshape(key_rows.shape[0], head_count, HEAD_DIM)
    value_heads = value_rows.reshape(value_rows.shape[0], head_count, HEAD_DIM)
    scores = jnp.einsum(
        "qhd,khd->hqk", query_heads, key_heads, preferred_element_type=jnp.float32
    ) * HEAD_DIM ** (-0.5)
    scores = jnp.where(key_mask[None, None, :], scores, NEGATIVE)
    new_max = jnp.maximum(row_max, jnp.max(scores, axis=2))
    shrink = jnp.exp(row_max - new_max)
    weights = jnp.exp(scores - new_max[:, :, None])
    weight_sum = weight_sum * shrink + jnp.sum(weights, axis=2)
    mixed_sum = mixed_sum * shrink[:, :, None] + jnp.einsum(
        "hqk,khd->hqd",
        weights.astype(jnp.bfloat16),
        value_heads,
        preferred_element_type=jnp.float32,
    )
    return (new_max, weight_sum, mixed_sum)


def gathered_attention(
    queries, keys, values, text_keys, text_values, prompt_lengths, frame_counts, n
):
    row_count, head_cols = queries.shape
    head_count = head_cols // HEAD_DIM
    all_counts = lax.all_gather(frame_counts, "seq", axis=0, tiled=True)
    query_heads = queries.reshape(row_count, head_count, HEAD_DIM)
    text_mask = jnp.arange(text_keys.shape[0], dtype=jnp.int32) < prompt_lengths[0]
    empty_state = (
        jnp.full((head_count, row_count), NEGATIVE, jnp.float32),
        jnp.zeros((head_count, row_count), jnp.float32),
        jnp.zeros((head_count, row_count, HEAD_DIM), jnp.float32),
    )
    text_state = attend_block(empty_state, text_keys, text_values, query_heads, text_mask)
    key_rows = lax.all_gather(keys, "seq", axis=0, tiled=True)
    value_rows = lax.all_gather(values, "seq", axis=0, tiled=True)
    positions = jnp.arange(key_rows.shape[0], dtype=jnp.int32)
    _, weight_sum, mixed_sum = attend_block(
        text_state, key_rows, value_rows, query_heads,
        frame_valid(positions, all_counts, row_count // frame_counts.shape[0]),
    )
    return (
        jnp.transpose(mixed_sum / weight_sum[:, :, None], (1, 0, 2))
        .reshape(row_count, head_cols)
        .astype(jnp.bfloat16)
    )


def fits_fused(n, cfgs, tps, queries, text_keys, frame_counts, out_weight):
    heads = queries.shape[2] // HEAD_DIM
    chips = n // CORES
    if cfgs != 2 or tps != 2 or n % CORES or frame_counts.shape[0] != 1:
        return False
    if chips != 4 or heads % chips or heads // chips < 4:
        return False
    if 3 * queries.shape[1] + 2 * text_keys.shape[1] > n * queries.shape[1]:
        return False
    return out_weight.shape[1] % (8 * HEAD_DIM) == 0 and queries.shape[1] % 16 == 0


def body(n, cfgs, tps, queries, keys, values, text_keys, text_values, prompt_lengths, frame_counts, out_weight):
    rows = queries.shape[1]
    if fits_fused(n, cfgs, tps, queries, text_keys, frame_counts, out_weight):
        return fused_step(
            queries[0], keys[0], values[0], text_keys[0], text_values[0],
            prompt_lengths, frame_counts, out_weight, n,
        )
    attended = gathered_attention(
        queries[0], keys[0], values[0], text_keys[0], text_values[0],
        prompt_lengths, frame_counts, n,
    )
    branch = lax.psum_scatter(
        lax.dot_general(
            out_weight, attended, (((0,), (1,)), ((), ())), preferred_element_type=jnp.float32
        ).astype(jnp.bfloat16),
        "tp",
        scatter_dimension=0,
        tiled=True,
    )
    half = branch.shape[0] // cfgs
    mine = lax.axis_index("cfg")
    kept = lax.dynamic_slice_in_dim(branch, mine * half, half, 0)
    given = lax.dynamic_slice_in_dim(branch, (1 - mine) * half, half, 0)
    other = lax.ppermute(given, "cfg", [(0, 1), (1, 0)])
    first = mine == 0
    conditional = jnp.where(first, kept, other).astype(jnp.float32)
    unconditional = jnp.where(first, other, kept).astype(jnp.float32)
    guided = unconditional + GUIDANCE * (conditional - unconditional)
    valid = (jnp.arange(rows, dtype=jnp.int32) < frame_counts[0])[None, :]

    def local_sum(field):
        return jnp.sum(jnp.where(valid, field, 0.0), axis=1)

    sums = lax.psum(
        jnp.stack([
            local_sum(guided),
            local_sum(guided * guided),
            local_sum(conditional),
            local_sum(conditional * conditional),
            jnp.full((half,), frame_counts[0].astype(jnp.float32)),
        ]),
        "seq",
    )
    means = sums[:4] / sums[4:5]
    guided_mean = means[0]
    guided_var = means[1] - guided_mean * guided_mean
    cond_var = means[3] - means[2] * means[2]
    std_ratio = jnp.sqrt((cond_var + 1.0) / (guided_var + 1.0))
    factor = RESCALE * std_ratio + (1.0 - RESCALE)
    velocity = guided_mean[:, None] + (guided - guided_mean[:, None]) * factor[:, None]
    return velocity.astype(jnp.bfloat16).T


def solution(mesh):
    placed = (
        P("cfg", "seq", "tp"),
        P("cfg", "seq", "tp"),
        P("cfg", "seq", "tp"),
        P("cfg", None, "tp"),
        P("cfg", None, "tp"),
        P("cfg"),
        P("seq"),
        P("tp", None),
    )
    return jax.shard_map(
        functools.partial(body, mesh.shape["seq"], mesh.shape["cfg"], mesh.shape["tp"]),
        mesh=mesh, in_specs=placed, out_specs=P("seq", ("tp", "cfg")), check_vma=False,
    )
```

time: 266 us -> 248 us (0.932)
  Pallas kernels: 261 us -> 244 us
    pallas_call x1, Pallas kernels: 261 us -> 244 us  [fused_step(): pl.pallas_call(functools.partial(step_kernel, n, chips, group, rows, text...]
where the time goes in v2:
time: 248 us
  Pallas kernels  244 us (98%)
    pallas_call x1, Pallas kernels, fused_step(): pl.pallas_call(functools.partial(step_kernel, n, chips, group, rows, text...  244 us

profile of v2, /device:TPU:0, one launch (start us, length us, event | category | flops | bytes accessed | tf_op | source)
XLA Modules:
  0.0 247.6 jit_solution(15266607431373195018)
XLA Ops:
  1.3 243.9 %shard_map.82 = bf16[480,1280]{1,0:T(8,128)(2,1)} custom-call(bf16[480,2560]{1,0:T(8,128)(2,1)} %bitcast.9, bf16[480,2560]{1,0:T(8,128)(2,1)} %bitcast.10, bf16[480,2560]{1,0:T(8,128)(2,1)} %bitcast.11, bf16[512,2560]{1,0:T(8,128)(2,1)} %bitcast.7, bf16[512,2560]{1,0:T(8,128)(2,1)} %bitcast.8, bf16[4,5,128,5120]{3,2,1,0:T(8,128)(2,1)} %bitcast.6, ...), custom_call_target="tpu_custom_call" | custom-call | tf_op jit(solution)/shard_map/pallas_call | solution.py:573
  245.2 2.4 copy.12

commit v3 on v2

--- a/solution.py
+++ b/solution.py
@@ -56,14 +56,19 @@
         return lax.rem(chip + step, chips)
 
     mid = chips // 2
-    late = mid - lax.div(chip, mid)
-    gap = lax.rem(chip + chips - late, chips)
+    upper = lax.div(chip, mid)
+    lower = 1 - upper
+    gap = lax.rem(upper * chip + lower * (chips - 1 - chip) + chips + 1 - mid, chips)
     at_end = lax.rem(chip, chips - 1) == 0
     inside = lax.rem(chip, chips - 1) != 0
 
     def source(place):
-        other = lax.rem(late + place + lax.div(place + chips - gap, chips), chips)
+        other = lax.rem(mid - 1 + place + lax.div(place + chips - gap, chips), chips)
+        other = upper * other + lower * (chips - 1 - other)
         return jnp.where(place == 0, chip, other)
+
+    def turned(step):
+        return upper * step + lower * (chips - step)
 
     def step_from(other):
         return lax.rem(chip + chips - other, chips)
@@ -152,9 +157,9 @@
             ob.at[head, chip], ab.at[c, t, head, chip], orecv.at[head, 0]
         )
 
-    def arrived(head, place, odd):
-        if place % 2 == odd:
-            return passed.at[head, place // (chips - 1)]
+    def arrived(head, place, turn):
+        if place // half == turn:
+            return passed.at[head, place]
         return direct.at[head]
 
     def x_copy(head, place):
@@ -166,7 +171,7 @@
         return across(piece, piece, send.at[head], arrived(head, place, 0), y_side)
 
     def relay(head, place):
-        if place % 2 == 0:
+        if place < half:
             piece = ab.at[1 - c, t, head, source(place)]
             side = x_side
         else:
@@ -219,12 +224,12 @@
 
     def start_kv(head):
         for step in range(1, chips):
-            for copy in kv_copies(head, step):
+            for copy in kv_copies(head, turned(step)):
                 copy.start()
 
     def start_q(head):
         for step in range(1, chips):
-            q_copy(head, step).start()
+            q_copy(head, turned(step)).start()
 
     for step in range(1, n):
         count_copy(step).start()
@@ -251,9 +256,9 @@
     lane = lax.broadcasted_iota(jnp.int32, (rows, HEAD_DIM), 1)
     place_in = lax.broadcasted_iota(jnp.int32, (rows, HEAD_DIM), 0)
 
-    def fill_bias(source, _):
-        limit = cb[source][0:1, :]
-        bias[slot(source), :] = jnp.where(
+    def fill_bias(origin, _):
+        limit = cb[origin][0:1, :]
+        bias[slot(origin), :] = jnp.where(
             (lane == 0) & (place_in >= limit), NEGATIVE, 0.0
         ).astype(bf16)
         return 0
@@ -303,8 +308,8 @@
     def take_keys(head):
         drain(kb.at[0, pl.ds(0, 3 * rows + 2 * text)], local.at[head])
         for step in range(1, chips):
-            drain(blocks_of(2), krecv.at[head, step - 1])
-            for copy in forwards(head, step):
+            drain(blocks_of(2), krecv.at[head, turned(step) - 1])
+            for copy in forwards(head, turned(step)):
                 copy.start()
         drain(blocks_of(n), frecv.at[head])
 
@@ -320,14 +325,10 @@
         for place in places:
             share_piece(head, place)
 
-    def pass_early(head):
-        drain(blocks_of(chips - 1), passed.at[head, 0])
-        for place in range(chips - 1):
+    def pass_on(head, places):
+        for place in places:
+            drain(blocks_of(1), passed.at[head, place])
             relay(head, place).start()
-
-    def pass_late(head):
-        drain(blocks_of(1), passed.at[head, 1])
-        relay(head, chips - 1).start()
 
     def blocks(head, after):
         def block(place, _):
@@ -374,7 +375,7 @@
 
     def product(head, branch, span):
         rows_in = jnp.concatenate(
-            [ab[branch, side, head, source] for side in range(2) for source in range(chips)],
+            [ab[branch, side, head, owner] for side in range(2) for owner in range(chips)],
             axis=1,
         )
         weight = wb[head, :, :, :, span].reshape(depth, part)
@@ -382,7 +383,7 @@
 
     def side_product(head, branch, side, span):
         rows_in = jnp.concatenate(
-            [ab[branch, side, head, source] for source in range(chips)], axis=1
+            [ab[branch, side, head, owner] for owner in range(chips)], axis=1
         )
         weight = wb[head, side, :, :, span].reshape(chips * HEAD_DIM, part)
         return jnp.dot(rows_in, weight, preferred_element_type=f32)
@@ -399,6 +400,14 @@
 
         lax.fori_loop(0, parts, one, 0)
 
+    def project_branch(head, branch):
+        def one(index, _):
+            span = span_of(index)
+            acc[branch, :, span] += product(head, branch, span)
+            return 0
+
+        lax.fori_loop(0, parts, one, 0)
+
     def project_side(head, branch, side):
         def one(index, _):
             span = span_of(index)
@@ -429,48 +438,51 @@
 
         @pl.when(head >= 1)
         def _():
-            pass_early(head - 1)
-            pass_late(head - 1)
-
-        @pl.when(head + 1 < last)
-        def _():
-            share(head, range(1, chips))
-
-        @pl.when(head == 1)
+            share(head - 1, range(1, chips))
+
+        @pl.when(head == 2)
         def _():
             drain(wb.at[:, 0], wsem.at[0])
             drain(wb.at[:, 0, near], wsem.at[2])
 
+        @pl.when(head >= 2)
+        def _():
+            collect(head - 2)
+            project(head - 2)
+
         @pl.when(head >= 1)
         def _():
-            collect(head - 1)
-            project(head - 1)
+            pass_on(head - 1, range(chips))
 
         return 0
 
     lax.fori_loop(0, last, one_head, 0)
-    share(last - 1, range(1, chips - 1))
+    early = range(1, chips - 1)
+    collect(last - 2)
+    project(last - 2)
+    share(last - 1, early)
+
     take_keys(last)
 
     def after_block(place):
         @pl.when(place == 0)
         def _():
             share_piece(last - 1, chips - 1)
-            pass_early(last - 1)
+            pass_on(last - 1, range(chips - 1))
 
         @pl.when(place == chips - 2)
         def _():
-            pass_late(last - 1)
+            pass_on(last - 1, (chips - 1,))
+            pass_on(last, (0,))
 
     blocks(last, after_block)
+    share(last, early)
     collect(last - 1)
     project(last - 1)
-    share(last, range(1, chips))
-    project_side(last, c, t)
-    pass_early(last)
-    pass_late(last)
+    share(last, (chips - 1,))
+    pass_on(last, range(1, chips))
     collect_direct(last)
-    project_side(last, c, 1 - t)
+    project_branch(last, c)
     project_side(last, 1 - c, t)
     collect_relayed(last)
 
@@ -479,8 +491,8 @@
     first = jnp.full((rows, part), c, jnp.int32) == 0
     pairs = part // HEAD_DIM
 
-    def guide(index, _):
-        span = span_of(index)
+    def guide(index):
+        span = pl.ds(index * part, part)
         mine = acc[c, :, span].astype(bf16).astype(f32)
         other = acc[1 - c, :, span] + side_product(last, 1 - c, 1 - t, span)
         other = other.astype(bf16).astype(f32)
@@ -499,16 +511,11 @@
                     :, pair * HEAD_DIM:(pair + 1) * HEAD_DIM
                 ]
 
-        @pl.when(index == parts - 2)
-        def _():
+    for index in range(parts):
+        guide(index)
+        if index >= parts - 2:
             for step in range(1, n):
-                stat_copy(0, step).start()
-
-        return 0
-
-    lax.fori_loop(0, parts, guide, 0)
-    for step in range(1, n):
-        stat_copy(1, step).start()
+                stat_copy(index + 2 - parts, step).start()
 
     def settle(head, _):
         drain(kb.at[pl.ds(0, chips)], send.at[head])
@@ -518,8 +525,8 @@
     drain(wb.at[:, 0], wsem.at[3])
     drain(cb.at[pl.ds(0, n - 1)], count.at[0])
     valid_total = cb[0][0:1, :]
-    for source in range(1, n):
-        valid_total = valid_total + cb[source][0:1, :]
+    for origin in range(1, n):
+        valid_total = valid_total + cb[origin][0:1, :]
     valid_total = valid_total.astype(f32)
 
     def store(index):
@@ -599,7 +606,7 @@
             dma((2,)),
             dma((group,)),
             dma((group, chips)),
-            dma((group, 2)),
+            dma((group, chips)),
             dma((group,)),
             dma((group,)),
             dma((4,)),
@@ -607,7 +614,7 @@
             dma((1,)),
         ],
         compiler_params=pltpu.CompilerParams(
-            collective_id=0, has_side_effects=True, vmem_limit_bytes=62 * 1024 * 1024
+            collective_id=0, has_side_effects=True, vmem_limit_bytes=52 * 1024 * 1024
         ),
     )(queries, keys, values, text_keys, text_values, weight, frame_counts, prompt_lengths)
 

time: 248 us -> 242 us (0.976)
  Pallas kernels: 244 us -> 240 us
    pallas_call x1, Pallas kernels: 244 us -> 240 us  [fused_step(): pl.pallas_call(functools.partial(step_kernel, n, chips, group, rows, text...]
where the time goes in v3:
time: 242 us
  Pallas kernels  240 us (99%)
    pallas_call x1, Pallas kernels, fused_step(): pl.pallas_call(functools.partial(step_kernel, n, chips, group, rows, text...  240 us

profile of v3, /device:TPU:0, one launch (start us, length us, event | category | flops | bytes accessed | tf_op | source)
XLA Modules:
  0.0 242.1 jit_solution(3080365309060680254)
XLA Ops:
  1.3 239.7 %shard_map.82 = bf16[480,1280]{1,0:T(8,128)(2,1)S(1)} custom-call(bf16[480,2560]{1,0:T(8,128)(2,1)} %bitcast.9, bf16[480,2560]{1,0:T(8,128)(2,1)} %bitcast.10, bf16[480,2560]{1,0:T(8,128)(2,1)} %bitcast.11, bf16[512,2560]{1,0:T(8,128)(2,1)} %bitcast.7, bf16[512,2560]{1,0:T(8,128)(2,1)} %bitcast.8, bf16[4,5,128,5120]{3,2,1,0:T(8,128)(2,1)} %bitcast.6, ...), custom_call_target="tpu_custom_call" | custom-call | tf_op jit(solution)/shard_map/pallas_call | solution.py:580
  241.0 1.0 copy.12

commit v4 on v3

--- a/solution.py
+++ b/solution.py
@@ -468,6 +468,9 @@
         @pl.when(place == 0)
         def _():
             share_piece(last - 1, chips - 1)
+
+        @pl.when(place == 1)
+        def _():
             pass_on(last - 1, range(chips - 1))
 
         @pl.when(place == chips - 2)

time: 242 us -> 242 us (level)
  no operation moved by 1% of the time
where the time goes in v4:
time: 242 us
  Pallas kernels  240 us (99%)
    pallas_call x1, Pallas kernels, fused_step(): pl.pallas_call(functools.partial(step_kernel, n, chips, group, rows, text...  240 us

profile of v4, /device:TPU:0, one launch (start us, length us, event | category | flops | bytes accessed | tf_op | source)
XLA Modules:
  0.0 242.1 jit_solution(11111961509918036182)
XLA Ops:
  1.3 239.7 %shard_map.82 = bf16[480,1280]{1,0:T(8,128)(2,1)S(1)} custom-call(bf16[480,2560]{1,0:T(8,128)(2,1)} %bitcast.9, bf16[480,2560]{1,0:T(8,128)(2,1)} %bitcast.10, bf16[480,2560]{1,0:T(8,128)(2,1)} %bitcast.11, bf16[512,2560]{1,0:T(8,128)(2,1)} %bitcast.7, bf16[512,2560]{1,0:T(8,128)(2,1)} %bitcast.8, bf16[4,5,128,5120]{3,2,1,0:T(8,128)(2,1)} %bitcast.6, ...), custom_call_target="tpu_custom_call" | custom-call | tf_op jit(solution)/shard_map/pallas_call | solution.py:583
  241.0 1.0 copy.12
